TPU v7x, 256 devices: a whole 4x4x8 slice. The times are simulated.
256 devices in a mesh: row: 8 (over y, x_hi), col: 32 (over z, x_lo, core).
Axes of the slice: x: 4 (x_hi: 2, x_lo: 2; x = x_hi * 2 + x_lo), y: 4, z: 8, core: 2. Of those that a mesh axis runs over, the one named last changes fastest.
Arguments:
- field: float32 [2, 2048, 16384], P(None, 'row', 'col'), may hold values from -4 to 4
- states: float32 [32, 256, 512], P('row', 'col'), may hold values from -1 to 1
- input_weight: bfloat16 [20736, 512], P('col'), may hold values from -0.0390625 to 0.0390625
- recurrent_weight: bfloat16 [512, 512], replicated, may hold values from -0.25 to 0.25
- bias: float32 [512], replicated, may hold values from -3 to 3
- output_weight: bfloat16 [512, 8192], P(None, 'col'), may hold values from -0.25 to 0.25
- model_gain: float32 [2, 64, 64], replicated, may hold values from 0.5 to 1.5
Outputs:
- prediction: float32 [2, 2048, 16384], P(None, 'row', 'col')
- fresh_states: float32 [32, 256, 512], P('row', 'col')
All inputs are finite; a program needn't handle non-finite values.
Results may differ from a plain program's by a relative error of at most 0.0033.
Values may be sent and summed in bfloat16 or wider, within the bound.
A program may use at most 64 MiB of HBM per device.

v0:
```python
import jax
import jax.numpy as jnp
from jax import lax
from jax.sharding import PartitionSpec as P

CORE = 64
MARGIN = 4
NODES = 512
PATCH = 72


dispersion = 2.0
nonlinear = -0.7
time_step = 0.1


def extended(array, sides, width):
    edges = {}
    for axis, dim in sides:
        size, length = (lax.axis_size(axis), array.shape[dim])
        up = [(i, (i + 1) % size) for i in range(size)]
        last = lax.slice_in_dim(array, length - width, length, axis=dim)
        leading = lax.slice_in_dim(array, 0, width, axis=dim)
        edges[dim] = (
            lax.ppermute(last, axis, up),
            lax.ppermute(leading, axis, [(b, a) for a, b in up]),
        )
    done = []
    for _, dim in sides:
        low, high = edges[dim]
        around = [(width, width) if d in done else (0, 0) for d in range(array.ndim)]
        array = jnp.concatenate([jnp.pad(low, around), array, jnp.pad(high, around)], axis=dim)
        done.append(dim)
    return array


def extended_2(cells, sides, width):
    for axis, dim in sides:
        count = lax.axis_size(axis)
        head = lax.slice_in_dim(cells, 0, width, axis=dim)
        tail = lax.slice_in_dim(cells, cells.shape[dim] - width, cells.shape[dim], axis=dim)
        cells = jnp.concatenate(
            [
                lax.ppermute(tail, axis, [(i, (i + 1) % count) for i in range(count)]),
                cells,
                lax.ppermute(head, axis, [((i + 1) % count, i) for i in range(count)]),
            ],
            axis=dim,
        )
    return cells


def cut_along(array, dim, length):
    before, after = (array.shape[:dim], array.shape[dim + 1 :])
    return jnp.moveaxis(array.reshape(*before, length, -1, *after), dim, 0)


def sum_at_owner(array, axis, dim):
    parts = cut_along(array, dim, lax.axis_size(axis))
    arrived = lax.all_to_all(parts, axis, split_axis=0, concat_axis=0, tiled=True)
    return arrived.sum(axis=0)


def reaction(center, spread):
    real_part = center[0]
    imag_part = center[1]
    modulus = real_part * real_part + imag_part * imag_part
    first = (
        real_part
        + spread[0]
        - dispersion * spread[1]
        - modulus * (real_part - nonlinear * imag_part)
    )
    second = (
        imag_part
        + spread[1]
        + dispersion * spread[0]
        - modulus * (imag_part + nonlinear * real_part)
    )
    return jnp.stack([first, second])


def shrunk_tendency(padded):
    center = padded[:, 1:-1, 1:-1]
    spread = (
        padded[:, :-2, 1:-1]
        + padded[:, 2:, 1:-1]
        + padded[:, 1:-1, :-2]
        + padded[:, 1:-1, 2:]
        - 4.0 * center
    )
    return reaction(center, spread)


def section_slope(values):
    padded = extended(values, (("row", 1), ("col", 2)), 1)
    return shrunk_tendency(padded)


def local(field, states, input_weight, recurrent_weight, bias, output_weight, model_gain):
    height = field.shape[1]
    width = field.shape[2]
    slope_one = section_slope(field)
    slope_two = section_slope(field + 0.5 * time_step * slope_one)
    slope_three = section_slope(field + 0.5 * time_step * slope_two)
    slope_four = section_slope(field + time_step * slope_three)
    model = field + time_step / 6.0 * (slope_one + 2.0 * slope_two + 2.0 * slope_three + slope_four)
    both = extended_2(
        jnp.concatenate([field, model], 0).astype(jnp.bfloat16), (("row", 1), ("col", 2)), MARGIN
    ).astype(jnp.float32)
    block_rows = height // CORE
    block_cols = width // CORE
    count = block_rows * block_cols
    pieces = [
        both[
            :,
            row_index * CORE : row_index * CORE + PATCH,
            col_index * CORE : col_index * CORE + PATCH,
        ]
        for row_index in range(block_rows)
        for col_index in range(block_cols)
    ]
    inputs = jnp.stack(pieces).reshape(count, -1).astype(jnp.bfloat16)
    previous = states.reshape(count, NODES).astype(jnp.bfloat16)
    recur = jnp.dot(previous, recurrent_weight, preferred_element_type=jnp.float32)
    moved = lax.all_to_all(inputs, "col", split_axis=1, concat_axis=0, tiled=True)
    drive = sum_at_owner(jnp.dot(moved, input_weight, preferred_element_type=jnp.float32), "col", 0)
    fresh = jnp.tanh(drive + recur + bias)
    readin = fresh.astype(jnp.bfloat16)
    readout = jnp.dot(
        readin,
        lax.all_gather(output_weight, "col", axis=1, tiled=True),
        preferred_element_type=jnp.float32,
    )
    placed = (
        readout.reshape(block_rows, block_cols, 2, CORE, CORE)
        .transpose(2, 0, 3, 1, 4)
        .reshape(2, height, width)
    )
    gained = (
        model.reshape(2, block_rows, CORE, block_cols, CORE) * model_gain[:, None, :, None, :]
    ).reshape(2, height, width)
    prediction = gained + placed
    return (prediction, fresh.reshape(block_rows, block_cols, NODES))


def solution(mesh):
    placed = (
        P(None, "row", "col"),
        P("row", "col", None),
        P("col", None),
        P(),
        P(),
        P(None, "col"),
        P(),
    )
    return jax.shard_map(
        local,
        mesh=mesh,
        in_specs=placed,
        out_specs=(P(None, "row", "col"), P("row", "col", None)),
        check_vma=False,
    )
```

profile of v0, /device:TPU:1, one launch (start us, length us, event | category | flops | bytes accessed | tf_op | source)
XLA Modules:
  0.0 252.5 jit_solution(5096580034369025727)
XLA Ops:
  8.7 3.6 %collective-permute-start = (f32[2,1,512]{2,1,0:T(1,128)S(1)}, f32[2,1,512]{2,1,0:T(1,128)S(1)}, u32[]{:S(2)}, u32[]{:S(2)}) collective-permute-start(f32[2,1,512]{2,1,0:T(1,128)S(1)} %get-tuple-element.64), channel_id=1, source_target_pairs={{0,32},{32,64},{64,96},{96,128},{128,160},{160,192},{192,224},{224... | collective-permute-start | bytes 12296 | tf_op jit(solution)/shard_map/ppermute | solution.py:25
  12.3 2.5 %collective-permute-start.1 = (f32[2,1,512]{2,1,0:T(1,128)S(1)}, f32[2,1,512]{2,1,0:T(1,128)S(1)}, u32[]{:S(2)}, u32[]{:S(2)}) collective-permute-start(f32[2,1,512]{2,1,0:T(1,128)S(1)} %get-tuple-element.65), channel_id=1, source_target_pairs={{32,0},{64,32},{96,64},{128,96},{160,128},{192,160},{224,192},{0,2... | collective-permute-start | bytes 12296 | tf_op jit(solution)/shard_map/ppermute | solution.py:26
  18.9 2.6 %collective-permute-done.2 = f32[2,256,1]{2,1,0:T(8,128)S(1)} collective-permute-done((f32[2,256,1]{2,1,0:T(8,128)S(1)}, f32[2,256,1]{2,1,0:T(8,128)S(1)}, u32[]{:S(2)}, u32[]{:S(2)}) %collective-permute-start.2) | collective-permute-done | bytes 2080 | tf_op jit(solution)/shard_map/ppermute | solution.py:25
  21.6 5.3 %collective-permute-done.3 = f32[2,256,1]{2,1,0:T(8,128)S(1)} collective-permute-done((f32[2,256,1]{2,1,0:T(8,128)S(1)}, f32[2,256,1]{2,1,0:T(8,128)S(1)}, u32[]{:S(2)}, u32[]{:S(2)}) %collective-permute-start.3) | collective-permute-done | bytes 2080 | tf_op jit(solution)/shard_map/ppermute | solution.py:26
  26.9 4.0 %fusion.24 = f32[2,256,512]{2,1,0:T(8,128)S(1)} fusion(f32[2,256,1]{2,1,0:T(8,128)S(1)} %collective-permute-done.3, f32[2,1,512]{2,1,0:T(1,128)S(1)} %collective-permute-done.1, f32[2,256,512]{2,1,0:T(8,128)} %param.7, f32[2,1,512]{2,1,0:T(1,128)S(1)} %collective-permute-done, f32[2,256,1]{2,1,0:T(8,128)S(1)} %collective-permute-done.2), kind=kLoop, calls=%fused_computation.50 | loop fusion | flops 4980736 | bytes 2109440 | tf_op jit(solution)/shard_map/sub | solution.py:86
  31.9 4.7 %collective-permute-start.5 = (f32[2,1,512]{2,1,0:T(1,128)S(1)}, f32[2,1,512]{2,1,0:T(1,128)S(1)}, u32[]{:S(2)}, u32[]{:S(2)}) collective-permute-start(f32[2,1,512]{2,1,0:T(1,128)S(1)} %get-tuple-element.61), channel_id=1, source_target_pairs={{32,0},{64,32},{96,64},{128,96},{160,128},{192,160},{224,192},{0,2... | collective-permute-start | bytes 12296 | tf_op jit(solution)/shard_map/ppermute | solution.py:26
  37.6 9.3 %collective-permute-done.6 = f32[2,256,1]{2,1,0:T(8,128)S(1)} collective-permute-done((f32[2,256,1]{2,1,0:T(8,128)S(1)}, f32[2,256,1]{2,1,0:T(8,128)S(1)}, u32[]{:S(2)}, u32[]{:S(2)}) %collective-permute-start.6) | collective-permute-done | bytes 2080 | tf_op jit(solution)/shard_map/ppermute | solution.py:25
  46.9 2.2 collective-permute-done.7
  50.5 5.1 %collective-permute-start.9 = (f32[2,1,512]{2,1,0:T(1,128)S(1)}, f32[2,1,512]{2,1,0:T(1,128)S(1)}, u32[]{:S(2)}, u32[]{:S(2)}) collective-permute-start(f32[2,1,512]{2,1,0:T(1,128)S(1)} %get-tuple-element.57), channel_id=1, source_target_pairs={{32,0},{64,32},{96,64},{128,96},{160,128},{192,160},{224,192},{0,2... | collective-permute-start | bytes 12296 | tf_op jit(solution)/shard_map/ppermute | solution.py:26
  56.6 11.2 %collective-permute-done.10 = f32[2,256,1]{2,1,0:T(8,128)S(1)} collective-permute-done((f32[2,256,1]{2,1,0:T(8,128)S(1)}, f32[2,256,1]{2,1,0:T(8,128)S(1)}, u32[]{:S(2)}, u32[]{:S(2)}) %collective-permute-start.10) | collective-permute-done | bytes 2080 | tf_op jit(solution)/shard_map/ppermute | solution.py:25
  69.2 5.1 %collective-permute-start.13 = (f32[2,1,512]{2,1,0:T(1,128)S(1)}, f32[2,1,512]{2,1,0:T(1,128)S(1)}, u32[]{:S(2)}, u32[]{:S(2)}) collective-permute-start(f32[2,1,512]{2,1,0:T(1,128)S(1)} %get-tuple-element.53), channel_id=1, source_target_pairs={{32,0},{64,32},{96,64},{128,96},{160,128},{192,160},{224,192},{0,2... | collective-permute-start | bytes 12296 | tf_op jit(solution)/shard_map/ppermute | solution.py:26
  74.4 3.1 %collective-permute-start.14 = (f32[2,256,1]{2,1,0:T(8,128)S(1)}, f32[2,256,1]{2,1,0:T(8,128)S(1)}, u32[]{:S(2)}, u32[]{:S(2)}) collective-permute-start(f32[2,256,1]{2,1,0:T(8,128)S(1)} %get-tuple-element.50), channel_id=1, source_target_pairs={{0,1},{1,2},{2,3},{3,4},{4,5},{5,6},{6,7},{7,8},{8,9},{9,10},{10,1... | collective-permute-start | bytes 6152 | tf_op jit(solution)/shard_map/ppermute | solution.py:25
  77.5 7.9 %collective-permute-done.14 = f32[2,256,1]{2,1,0:T(8,128)S(1)} collective-permute-done((f32[2,256,1]{2,1,0:T(8,128)S(1)}, f32[2,256,1]{2,1,0:T(8,128)S(1)}, u32[]{:S(2)}, u32[]{:S(2)}) %collective-permute-start.14) | collective-permute-done | bytes 2080 | tf_op jit(solution)/shard_map/ppermute | solution.py:25
  92.1 2.4 collective-permute-start.16
  100.4 2.4 collective-permute-start.18
  115.3 9.9 %stack.155 = bf16[32,32,648]{2,0,1:T(8,128)(2,1)S(1)} concatenate(bf16[1,32,648]{2,0,1:T(2,128)(2,1)S(1)} %stack.156, bf16[1,32,648]{2,0,1:T(2,128)(2,1)} %stack.157, bf16[1,32,648]{2,0,1:T(2,128)(2,1)S(1)} %stack.158, bf16[1,32,648]{2,0,1:T(2,128)(2,1)S(1)} %stack.159, bf16[1,32,648]{2,0,1:T(2,128)(2,1)S(1)} %stack.160, bf16[1,32,648]{2,0,1:T(2,128)(2,1)} %stack.161, ...), dimensions={0} | concatenate | bytes 2654208 | tf_op jit(solution)/shard_map/stack | solution.py:123
  125.2 47.8 %all_to_all.18 = bf16[32,32,648]{2,0,1:T(8,128)(2,1)S(1)} all-to-all(bf16[32,32,648]{2,0,1:T(8,128)(2,1)S(1)} %stack.155), channel_id=1, replica_groups=mesh['row'=8,'col'=32] {'col'}, dimensions={1} | all-to-all | bytes 2654208 | tf_op jit(solution)/shard_map/all_to_all | solution.py:126
  173.0 2.3 fusion
  175.3 4.9 %all-to-all-start.1 = ((f32[32,32,512]{2,1,0:T(8,128)}), f32[32,32,512]{2,1,0:T(8,128)S(1)}, u32[]{:S(2)}, u32[]{:S(2)}) async-start(f32[32,32,512]{2,1,0:T(8,128)} %fusion), calls=%async_computation.1 | async-start | bytes 4194304 | tf_op jit(solution)/shard_map/all_to_all | solution.py:60
  181.7 2.7 %mul.228 = f32[2,256,512]{2,1,0:T(8,128)} reshape(f32[2,4,64,8,64]{4,3,2,1,0:T(8,128)} %mul.227) | data formatting | bytes 2097152 | tf_op jit(solution)/shard_map/mul | solution.py:141
  184.5 45.7 %all-to-all-done.1 = f32[32,32,512]{2,1,0:T(8,128)S(1)} async-done(((f32[32,32,512]{2,1,0:T(8,128)}), f32[32,32,512]{2,1,0:T(8,128)S(1)}, u32[]{:S(2)}, u32[]{:S(2)}) %all-to-all-start.1) | async-done | bytes 2097184 | tf_op jit(solution)/shard_map/all_to_all | solution.py:60
  230.6 5.9 %fusion.32 = f32[32,8192]{1,0:T(8,128)} fusion(bf16[512,8192]{1,0:T(8,128)(2,1)} %all-gather.2.cloned.1.call-done, f32[32,512]{1,0:T(8,128)S(1)} %fusion.3), kind=kOutput, calls=%fused_computation.131 | convolution fusion | flops 268451840 | bytes 9502720 | tf_op jit(solution)/shard_map/dot_general | solution.py:130
  238.5 2.5 %copy.42 = f32[2,4,64,8,64]{4,3,2,1,0:T(8,128)} copy(f32[2,4,64,8,64]{4,2,0,3,1:T(8,128)S(1)} %bitcast.17) | data formatting | bytes 2097152 | tf_op jit(solution)/shard_map/transpose | solution.py:137
  243.1 2.6 %multiply_add_fusion = f32[2,256,512]{2,1,0:T(8,128)} fusion(f32[2,256,512]{2,1,0:T(8,128)S(1)} %reshape.188, f32[2,256,512]{2,1,0:T(8,128)} %get-tuple-element.3, f32[2,256,512]{2,1,0:T(8,128)S(1)} %copy-done.2), kind=kLoop, calls=%fused_computation.69 | loop fusion | flops 524288 | bytes 4194304 | tf_op jit(solution)/shard_map/add | solution.py:143
  (109 shorter events, 42.4 us)
Async XLA Ops:
  7.2 165.8 %copy-start = (bf16[648,512]{1,0:T(8,128)(2,1)S(1)}, bf16[648,512]{1,0:T(8,128)(2,1)}, u32[]{:S(2)}) copy-start(bf16[648,512]{1,0:T(8,128)(2,1)} %param.9) | copy-start | bytes 1990660
  7.2 223.4 %all-gather.2.cloned.1.call-start = ((), (), s32[]{:S(2)}) async-start(), calls=%async_computation.2 | async-start | bytes 8650752 | tf_op jit(solution)/shard_map/all_gather | solution.py:132
  8.7 18.1 %collective-permute-start = (f32[2,1,512]{2,1,0:T(1,128)S(1)}, f32[2,1,512]{2,1,0:T(1,128)S(1)}, u32[]{:S(2)}, u32[]{:S(2)}) collective-permute-start(f32[2,1,512]{2,1,0:T(1,128)S(1)} %get-tuple-element.64), channel_id=1, source_target_pairs={{0,32},{32,64},{64,96},{96,128},{128,160},{160,192},{192,224},{224... | collective-permute-start | bytes 12296 | tf_op jit(solution)/shard_map/ppermute | solution.py:25
  12.3 14.5 %collective-permute-start.1 = (f32[2,1,512]{2,1,0:T(1,128)S(1)}, f32[2,1,512]{2,1,0:T(1,128)S(1)}, u32[]{:S(2)}, u32[]{:S(2)}) collective-permute-start(f32[2,1,512]{2,1,0:T(1,128)S(1)} %get-tuple-element.65), channel_id=1, source_target_pairs={{32,0},{64,32},{96,64},{128,96},{160,128},{192,160},{224,192},{0,2... | collective-permute-start | bytes 12296 | tf_op jit(solution)/shard_map/ppermute | solution.py:26
  16.0 5.5 %collective-permute-start.2 = (f32[2,256,1]{2,1,0:T(8,128)S(1)}, f32[2,256,1]{2,1,0:T(8,128)S(1)}, u32[]{:S(2)}, u32[]{:S(2)}) collective-permute-start(f32[2,256,1]{2,1,0:T(8,128)S(1)} %get-tuple-element.62), channel_id=1, source_target_pairs={{0,1},{1,2},{2,3},{3,4},{4,5},{5,6},{6,7},{7,8},{8,9},{9,10},{10,1... | collective-permute-start | bytes 6152 | tf_op jit(solution)/shard_map/ppermute | solution.py:25
  18.2 8.6 %collective-permute-start.3 = (f32[2,256,1]{2,1,0:T(8,128)S(1)}, f32[2,256,1]{2,1,0:T(8,128)S(1)}, u32[]{:S(2)}, u32[]{:S(2)}) collective-permute-start(f32[2,256,1]{2,1,0:T(8,128)S(1)} %get-tuple-element.63), channel_id=1, source_target_pairs={{1,0},{2,1},{3,2},{4,3},{5,4},{6,5},{7,6},{8,7},{9,8},{10,9},{11,1... | collective-permute-start | bytes 6152 | tf_op jit(solution)/shard_map/ppermute | solution.py:26
  31.5 17.7 %collective-permute-start.4 = (f32[2,1,512]{2,1,0:T(1,128)S(1)}, f32[2,1,512]{2,1,0:T(1,128)S(1)}, u32[]{:S(2)}, u32[]{:S(2)}) collective-permute-start(f32[2,1,512]{2,1,0:T(1,128)S(1)} %get-tuple-element.60), channel_id=1, source_target_pairs={{0,32},{32,64},{64,96},{96,128},{128,160},{160,192},{192,224},{224... | collective-permute-start | bytes 12296 | tf_op jit(solution)/shard_map/ppermute | solution.py:25
  31.9 17.2 %collective-permute-start.5 = (f32[2,1,512]{2,1,0:T(1,128)S(1)}, f32[2,1,512]{2,1,0:T(1,128)S(1)}, u32[]{:S(2)}, u32[]{:S(2)}) collective-permute-start(f32[2,1,512]{2,1,0:T(1,128)S(1)} %get-tuple-element.61), channel_id=1, source_target_pairs={{32,0},{64,32},{96,64},{128,96},{160,128},{192,160},{224,192},{0,2... | collective-permute-start | bytes 12296 | tf_op jit(solution)/shard_map/ppermute | solution.py:26
  36.8 10.1 %collective-permute-start.6 = (f32[2,256,1]{2,1,0:T(8,128)S(1)}, f32[2,256,1]{2,1,0:T(8,128)S(1)}, u32[]{:S(2)}, u32[]{:S(2)}) collective-permute-start(f32[2,256,1]{2,1,0:T(8,128)S(1)} %get-tuple-element.58), channel_id=1, source_target_pairs={{0,1},{1,2},{2,3},{3,4},{4,5},{5,6},{6,7},{7,8},{8,9},{9,10},{10,1... | collective-permute-start | bytes 6152 | tf_op jit(solution)/shard_map/ppermute | solution.py:25
  37.3 11.8 %collective-permute-start.7 = (f32[2,256,1]{2,1,0:T(8,128)S(1)}, f32[2,256,1]{2,1,0:T(8,128)S(1)}, u32[]{:S(2)}, u32[]{:S(2)}) collective-permute-start(f32[2,256,1]{2,1,0:T(8,128)S(1)} %get-tuple-element.59), channel_id=1, source_target_pairs={{1,0},{2,1},{3,2},{4,3},{5,4},{6,5},{7,6},{8,7},{9,8},{10,9},{11,1... | collective-permute-start | bytes 6152 | tf_op jit(solution)/shard_map/ppermute | solution.py:26
  50.4 17.4 %collective-permute-start.8 = (f32[2,1,512]{2,1,0:T(1,128)S(1)}, f32[2,1,512]{2,1,0:T(1,128)S(1)}, u32[]{:S(2)}, u32[]{:S(2)}) collective-permute-start(f32[2,1,512]{2,1,0:T(1,128)S(1)} %get-tuple-element.56), channel_id=1, source_target_pairs={{0,32},{32,64},{64,96},{96,128},{128,160},{160,192},{192,224},{224... | collective-permute-start | bytes 12296 | tf_op jit(solution)/shard_map/ppermute | solution.py:25
  50.5 17.3 %collective-permute-start.9 = (f32[2,1,512]{2,1,0:T(1,128)S(1)}, f32[2,1,512]{2,1,0:T(1,128)S(1)}, u32[]{:S(2)}, u32[]{:S(2)}) collective-permute-start(f32[2,1,512]{2,1,0:T(1,128)S(1)} %get-tuple-element.57), channel_id=1, source_target_pairs={{32,0},{64,32},{96,64},{128,96},{160,128},{192,160},{224,192},{0,2... | collective-permute-start | bytes 12296 | tf_op jit(solution)/shard_map/ppermute | solution.py:26
  55.7 12.1 %collective-permute-start.10 = (f32[2,256,1]{2,1,0:T(8,128)S(1)}, f32[2,256,1]{2,1,0:T(8,128)S(1)}, u32[]{:S(2)}, u32[]{:S(2)}) collective-permute-start(f32[2,256,1]{2,1,0:T(8,128)S(1)} %get-tuple-element.54), channel_id=1, source_target_pairs={{0,1},{1,2},{2,3},{3,4},{4,5},{5,6},{6,7},{7,8},{8,9},{9,10},{10,1... | collective-permute-start | bytes 6152 | tf_op jit(solution)/shard_map/ppermute | solution.py:25
  56.6 11.2 %collective-permute-start.11 = (f32[2,256,1]{2,1,0:T(8,128)S(1)}, f32[2,256,1]{2,1,0:T(8,128)S(1)}, u32[]{:S(2)}, u32[]{:S(2)}) collective-permute-start(f32[2,256,1]{2,1,0:T(8,128)S(1)} %get-tuple-element.55), channel_id=1, source_target_pairs={{1,0},{2,1},{3,2},{4,3},{5,4},{6,5},{7,6},{8,7},{9,8},{10,9},{11,1... | collective-permute-start | bytes 6152 | tf_op jit(solution)/shard_map/ppermute | solution.py:26
  69.1 17.4 %collective-permute-start.12 = (f32[2,1,512]{2,1,0:T(1,128)S(1)}, f32[2,1,512]{2,1,0:T(1,128)S(1)}, u32[]{:S(2)}, u32[]{:S(2)}) collective-permute-start(f32[2,1,512]{2,1,0:T(1,128)S(1)} %get-tuple-element.52), channel_id=1, source_target_pairs={{0,32},{32,64},{64,96},{96,128},{128,160},{160,192},{192,224},{224... | collective-permute-start | bytes 12296 | tf_op jit(solution)/shard_map/ppermute | solution.py:25
  69.2 17.3 %collective-permute-start.13 = (f32[2,1,512]{2,1,0:T(1,128)S(1)}, f32[2,1,512]{2,1,0:T(1,128)S(1)}, u32[]{:S(2)}, u32[]{:S(2)}) collective-permute-start(f32[2,1,512]{2,1,0:T(1,128)S(1)} %get-tuple-element.53), channel_id=1, source_target_pairs={{32,0},{64,32},{96,64},{128,96},{160,128},{192,160},{224,192},{0,2... | collective-permute-start | bytes 12296 | tf_op jit(solution)/shard_map/ppermute | solution.py:26
  74.4 11.0 %collective-permute-start.14 = (f32[2,256,1]{2,1,0:T(8,128)S(1)}, f32[2,256,1]{2,1,0:T(8,128)S(1)}, u32[]{:S(2)}, u32[]{:S(2)}) collective-permute-start(f32[2,256,1]{2,1,0:T(8,128)S(1)} %get-tuple-element.50), channel_id=1, source_target_pairs={{0,1},{1,2},{2,3},{3,4},{4,5},{5,6},{6,7},{7,8},{8,9},{9,10},{10,1... | collective-permute-start | bytes 6152 | tf_op jit(solution)/shard_map/ppermute | solution.py:25
  77.5 9.0 %collective-permute-start.15 = (f32[2,256,1]{2,1,0:T(8,128)S(1)}, f32[2,256,1]{2,1,0:T(8,128)S(1)}, u32[]{:S(2)}, u32[]{:S(2)}) collective-permute-start(f32[2,256,1]{2,1,0:T(8,128)S(1)} %get-tuple-element.51), channel_id=1, source_target_pairs={{1,0},{2,1},{3,2},{4,3},{5,4},{6,5},{7,6},{8,7},{9,8},{10,9},{11,1... | collective-permute-start | bytes 6152 | tf_op jit(solution)/shard_map/ppermute | solution.py:26
  89.1 5.4 %collective-permute-start.17 = (bf16[4,4,512]{2,1,0:T(4,128)(2,1)S(1)}, bf16[4,4,512]{2,1,0:T(4,128)(2,1)S(1)}, u32[]{:S(2)}, u32[]{:S(2)}) collective-permute-start(bf16[4,4,512]{2,1,0:T(4,128)(2,1)S(1)} %get-tuple-element.47), channel_id=1, source_target_pairs={{32,0},{64,32},{96,64},{128,96},{160,128},{192,160},{224,192},{0,2... | collective-permute-start | bytes 49160 | tf_op jit(solution)/shard_map/ppermute | solution.py:46
  92.1 7.3 %collective-permute-start.16 = (bf16[4,4,512]{2,1,0:T(4,128)(2,1)S(1)}, bf16[4,4,512]{2,1,0:T(4,128)(2,1)S(1)}, u32[]{:S(2)}, u32[]{:S(2)}) collective-permute-start(bf16[4,4,512]{2,1,0:T(4,128)(2,1)S(1)} %get-tuple-element.46), channel_id=1, source_target_pairs={{0,32},{32,64},{64,96},{96,128},{128,160},{160,192},{192,224},{224... | collective-permute-start | bytes 49160 | tf_op jit(solution)/shard_map/ppermute | solution.py:44
  100.4 7.2 %collective-permute-start.19 = (bf16[4,264,4]{2,1,0:T(8,128)(2,1)}, bf16[4,264,4]{2,1,0:T(8,128)(2,1)S(1)}, u32[]{:S(2)}, u32[]{:S(2)}) collective-permute-start(bf16[4,264,4]{2,1,0:T(8,128)(2,1)} %get-tuple-element.20), channel_id=1, source_target_pairs={{1,0},{2,1},{3,2},{4,3},{5,4},{6,5},{7,6},{8,7},{9,8},{10,9},{11,1... | collective-permute-start | bytes 25352 | tf_op jit(solution)/shard_map/ppermute | solution.py:46
  100.4 10.6 %collective-permute-start.18 = (bf16[4,264,4]{2,1,0:T(8,128)(2,1)}, bf16[4,264,4]{2,1,0:T(8,128)(2,1)S(1)}, u32[]{:S(2)}, u32[]{:S(2)}) collective-permute-start(bf16[4,264,4]{2,1,0:T(8,128)(2,1)} %get-tuple-element.21), channel_id=1, source_target_pairs={{0,1},{1,2},{2,3},{3,4},{4,5},{5,6},{6,7},{7,8},{8,9},{9,10},{10,1... | collective-permute-start | bytes 25352 | tf_op jit(solution)/shard_map/ppermute | solution.py:44
  175.3 54.9 %all-to-all-start.1 = ((f32[32,32,512]{2,1,0:T(8,128)}), f32[32,32,512]{2,1,0:T(8,128)S(1)}, u32[]{:S(2)}, u32[]{:S(2)}) async-start(f32[32,32,512]{2,1,0:T(8,128)} %fusion), calls=%async_computation.1 | async-start | bytes 4194304 | tf_op jit(solution)/shard_map/all_to_all | solution.py:60
  181.7 48.6 %copy-start.7 = (f32[512]{0:T(512)S(1)}, f32[512]{0:T(512)}, u32[]{:S(2)}) copy-start(f32[512]{0:T(512)} %param.11) | copy-start | bytes 6148
  (6 other events, 133.8 us)
Sparse Core Ops, SparseCore 0:
  9.8 104.8 all-gather.1
where the time goes:
time: 254 us; the launch traced here: 253 us
  waiting for transfers between devices  87.4 us (34%)
  blocking collectives  47.8 us (19%)
  local copies, waits for them, and re-layouts  40 us (16%)
  starting transfers between devices  39.9 us (16%)
  other arithmetic  14.7 us (6%)
  between operations  14.4 us (6%)
  matrix products  8.39 us (3%)
    all_to_all x1, blocking collectives, local(): lax.all_to_all(inputs, 'col', split_axis=1, concat_axis=0, tiled=True)  47.8 us
    all_to_all x1, waiting for transfers between devices, sum_at_owner(): lax.all_to_all(parts, axis, split_axis=0, concat_axis=0, tiled=True)  45.7 us
    ppermute x8, waiting for transfers between devices, extended(): lax.ppermute(last, axis, up)  31 us
    another operation x33, local copies, waits for them, and re-layouts, local(): inputs = jnp.stack(pieces).reshape(count, -1).astype(jnp.bfloat16)  26.7 us
    ppermute x8, starting transfers between devices, extended(): lax.ppermute(leading, axis, [(b, a) for a, b in up])  18.5 us
    ppermute x8, starting transfers between devices, extended(): lax.ppermute(last, axis, up)  11 us
    ppermute x8, waiting for transfers between devices, extended(): lax.ppermute(leading, axis, [(b, a) for a, b in up])  8.62 us
    sub x4, other arithmetic, shrunk_tendency(): padded[:, :-2, 1:-1] + padded[:, 2:, 1:-1] + padded[:, 1:-1, :-2]  6.1 us
  transfers between devices with their start and end apart: 22, of which 9 were waited for; matrix products, arithmetic and copies ran while one was open for 19% of the time, Pallas kernels for 0%

commit v1 on v0

v1 whole, which is shorter than its diff:
```python
import jax
import jax.numpy as jnp
from jax import lax
from jax.experimental import pallas as pl
from jax.experimental.pallas import tpu as pltpu
from jax.sharding import PartitionSpec as P

CORE = 64
MARGIN = 4
NODES = 512
PATCH = 72
MESH = pl.DeviceIdType.MESH

dispersion = 2.0
nonlinear = -0.7
time_step = 0.1

TILES = 5
ROWS = 296
TOP = 20
BF = jnp.bfloat16
F32 = jnp.float32


def lane_index(rows):
    return lax.broadcasted_iota(jnp.int32, (rows, 128), 1)


def reaction(re, im, lap_re, lap_im):
    modulus = re * re + im * im
    first = re + lap_re - dispersion * lap_im - modulus * (re - nonlinear * im)
    second = im + lap_im + dispersion * lap_re - modulus * (im + nonlinear * re)
    return first, second


def forecast_kernel(
    field, patches, model,
    left_out, right_out, left_in, right_in, top_in, bottom_in, corners,
    start, ping, pong, total, main, shifted, send_sem, recv_sem,
):
    row, col = lax.axis_index("row"), lax.axis_index("col")
    up, down = lax.rem(row + 7, 8), lax.rem(row + 1, 8)
    left, right = lax.rem(col + 31, 32), lax.rem(col + 1, 32)
    around = [(up, left), (up, col), (up, right), (row, left), (row, right), (down, left), (down, col), (down, right)]
    barrier = pltpu.get_barrier_semaphore()
    for device in around:
        pl.semaphore_signal(barrier, inc=1, device_id=device, device_id_type=MESH)
    lanes = lane_index(16)
    group = lanes // 8
    for ch in range(2):
        for side, buffer in ((0, left_out), (1, right_out)):
            packed = jnp.zeros((16, 128), F32)
            for k in range(16):
                tile = field[ch, 16 * k : 16 * k + 16, 384 * side : 384 * side + 128]
                shift = (8 * k + 8 * side) % 128
                moved = tile if shift == 0 else pltpu.roll(tile, shift, 1)
                packed = jnp.where(group == k, moved, packed)
            buffer[ch] = packed
    pl.semaphore_wait(barrier, 8)

    def copy(index, source, target, device):
        return pltpu.make_async_remote_copy(
            src_ref=source, dst_ref=target, send_sem=send_sem.at[index], recv_sem=recv_sem.at[index],
            device_id=device, device_id_type=MESH,
        )

    copies = [
        copy(0, field.at[:, 0:8, 0:128], corners.at[3], around[0]),
        copy(1, field.at[:, 0:8, :], bottom_in, around[1]),
        copy(2, field.at[:, 0:8, 384:512], corners.at[2], around[2]),
        copy(3, left_out, right_in, around[3]),
        copy(4, right_out, left_in, around[4]),
        copy(5, field.at[:, 248:256, 0:128], corners.at[1], around[5]),
        copy(6, field.at[:, 248:256, :], top_in, around[6]),
        copy(7, field.at[:, 248:256, 384:512], corners.at[0], around[7]),
    ]
    for one in copies:
        one.start()
    for one in copies:
        one.wait()

    def assemble(tiles, left_tile, right_tile, lane):
        moved = [pltpu.roll(tile, 4, 1) for tile in tiles]
        first = jnp.where(lane < 4, left_tile, moved[0])
        middle = [jnp.where(lane < 4, moved[t - 1], moved[t]) for t in (1, 2, 3)]
        last = jnp.where(lane < 4, moved[3], jnp.where(lane >= 124, left_tile, right_tile))
        return [first, *middle, last]

    short = lane_index(8)
    for ch in range(2):
        for k in range(16):
            tiles = [field[ch, 16 * k : 16 * k + 16, 128 * t : 128 * t + 128] for t in range(4)]
            left_tile = pltpu.roll(left_in[ch], (-8 * k - 4) % 128, 1)
            right_shift = (4 - 8 * k) % 128
            right_tile = pltpu.roll(right_in[ch], right_shift, 1)
            for t, tile in enumerate(assemble(tiles, left_tile, right_tile, lanes)):
                start[ch, t, TOP + 16 * k : TOP + 16 * k + 16, :] = tile
        for first_row, rows, at in ((TOP - 8, top_in, 0), (TOP + 256, bottom_in, 2)):
            tiles = [rows[ch, :, 128 * t : 128 * t + 128] for t in range(4)]
            left_tile = pltpu.roll(corners[at, ch], 4, 1)
            right_tile = pltpu.roll(corners[at + 1, ch], 4, 1)
            for t, tile in enumerate(assemble(tiles, left_tile, right_tile, short)):
                start[ch, t, first_row : first_row + 8, :] = tile

    def stage(source, finish):
        def block(i, carry):
            for sub in range(5):
                at = pl.multiple_of(8 + 40 * i + 8 * sub, 8)
                center = [[source[ch, t, pl.ds(at, 8), :] for t in range(TILES)] for ch in range(2)]
                laps = []
                for ch in range(2):
                    back = [pltpu.roll(tile, 1, 1) for tile in center[ch]]
                    ahead = [pltpu.roll(tile, 127, 1) for tile in center[ch]]
                    row_laps = []
                    for t in range(TILES):
                        before = jnp.where(short == 0, back[t - 1], back[t])
                        after = jnp.where(short == 127, ahead[(t + 1) % TILES], ahead[t])
                        above = source[ch, t, pl.ds(at - 1, 8), :]
                        below = source[ch, t, pl.ds(at + 1, 8), :]
                        row_laps.append(above + below + before + after - 4.0 * center[ch][t])
                    laps.append(row_laps)
                for t in range(TILES):
                    slopes = reaction(center[0][t], center[1][t], laps[0][t], laps[1][t])
                    for ch in range(2):
                        finish((ch, t, pl.ds(at, 8)), slopes[ch])
            return carry

        lax.fori_loop(0, 7, block, 0)

    def first_stage(at, slope):
        total[at] = slope
        ping[at] = start[at] + 0.5 * time_step * slope

    def second_stage(at, slope):
        total[at] = total[at] + 2.0 * slope
        pong[at] = start[at] + 0.5 * time_step * slope

    def third_stage(at, slope):
        total[at] = total[at] + 2.0 * slope
        ping[at] = start[at] + time_step * slope

    def fourth_stage(at, slope):
        pong[at] = start[at] + time_step / 6.0 * (total[at] + slope)

    stage(start, first_stage)
    stage(ping, second_stage)
    stage(pong, third_stage)
    stage(ping, fourth_stage)

    for channel in range(4):
        source, ch = (start, channel) if channel < 2 else (pong, channel - 2)

        def gather(i, carry):
            for a in range(4):
                at = pl.multiple_of(64 * a + 16 + 8 * i, 8)
                tiles = [source[ch, t, pl.ds(at, 8), :] for t in range(TILES)]
                for j in range(4):
                    main[pl.ds(128 * i + 4 * a + j, 8, stride=16), :] = tiles[j]
                    shifted[pl.ds(128 * i + 4 * a + j, 8, stride=16), :] = tiles[j + 1]
            return carry

        lax.fori_loop(0, 9, gather, 0)

        def pack(q, carry):
            at = pl.multiple_of(144 * q, 16)
            patches[8 * channel + q, 0:9] = main[pl.ds(at, 144), :].reshape(9, 16, 128).astype(BF)
            tail = jnp.zeros((16, 128), F32)
            for y in range(9):
                tile = shifted[pl.ds(pl.multiple_of(at + 16 * y, 16), 16), :]
                moved = tile if y == 0 else pltpu.roll(tile, 8 * y, 1)
                tail = jnp.where(group == y, moved, tail)
            patches[8 * channel + q, 9] = tail.astype(BF)
            return carry

        lax.fori_loop(0, 8, pack, 0)

    for ch in range(2):
        for k in range(16):
            tiles = [pltpu.roll(pong[ch, t, TOP + 16 * k : TOP + 16 * k + 16, :], 124, 1) for t in range(TILES)]
            for t in range(4):
                model[ch, 16 * k : 16 * k + 16, 128 * t : 128 * t + 128] = jnp.where(lanes < 124, tiles[t], tiles[t + 1])


def forecast(field):
    vmem = pl.BlockSpec(memory_space=pltpu.VMEM)
    block = pltpu.VMEM((2, TILES, ROWS, 128), F32)
    return pl.pallas_call(
        forecast_kernel,
        name="forecast",
        out_shape=(
            jax.ShapeDtypeStruct((32, 10, 16, 128), BF),
            jax.ShapeDtypeStruct((2, 256, 512), F32),
        ),
        in_specs=[vmem],
        out_specs=(vmem, vmem),
        scratch_shapes=[
            pltpu.VMEM((2, 16, 128), F32),
            pltpu.VMEM((2, 16, 128), F32),
            pltpu.VMEM((2, 16, 128), F32),
            pltpu.VMEM((2, 16, 128), F32),
            pltpu.VMEM((2, 8, 512), F32),
            pltpu.VMEM((2, 8, 512), F32),
            pltpu.VMEM((4, 2, 8, 128), F32),
            block,
            block,
            block,
            block,
            pltpu.VMEM((1152, 128), F32),
            pltpu.VMEM((1152, 128), F32),
            pltpu.SemaphoreType.DMA((8,)),
            pltpu.SemaphoreType.DMA((8,)),
        ],
        compiler_params=pltpu.CompilerParams(collective_id=0, has_side_effects=True),
    )(field)


def reservoir_kernel(
    patches, model, win, wout, wrec, bias, states, gain,
    prediction, fresh,
    rows, weights, wide, readout_weights, arrived, partial, partials, mine, readin, pieces, returned, placed,
    z_send, z_recv, z_local, d2d_send, d2d_recv, in_send, in_recv, drive_send, drive_recv,
    readin_send, readin_recv, out_send, out_recv,
):
    row, col = lax.axis_index("row"), lax.axis_index("col")
    z, x_lo, core = col // 4, lax.rem(col // 2, 2), lax.rem(col, 2)
    me = 2 * row + x_lo
    other_core = (row, col + 1 - 2 * core)
    hop = lax.rem(row + 4 * core, 8)
    z_source, z_target = lax.rem(z + hop, 8), lax.rem(z + 8 - hop, 8)
    source_device = (row, 4 * z_source + 2 * x_lo + core)
    target_device = (row, 4 * z_target + 2 * x_lo + core)

    def peer(i):
        index = lax.rem(me + i, 16)
        return index, (index // 2, 4 * z + 2 * lax.rem(index, 2) + core)

    def shard(index, kind):
        plane = lax.rem(z + index // 2 + 4 * kind, 8)
        return 4 * plane + 2 * lax.rem(index, 2) + kind

    barrier = pltpu.get_barrier_semaphore()

    def greet(i, carry):
        _, device = peer(i)
        pl.semaphore_signal(barrier, inc=1, device_id=device, device_id_type=MESH)
        return carry

    lax.fori_loop(1, 16, greet, 0)
    pl.semaphore_signal(barrier, inc=1, device_id=other_core, device_id_type=MESH)

    @pl.when(hop != 0)
    def _():
        pl.semaphore_signal(barrier, inc=1, device_id=source_device, device_id_type=MESH)
        pl.semaphore_signal(barrier, inc=1, device_id=target_device, device_id_type=MESH)

    pl.semaphore_wait(barrier, 16 + 2 * jnp.minimum(hop, 1))

    def remote(source, target, send_sem, recv_sem, device):
        return pltpu.make_async_remote_copy(
            src_ref=source, dst_ref=target, send_sem=send_sem, recv_sem=recv_sem, device_id=device, device_id_type=MESH
        )

    z_copies = [
        remote(win, weights.at[core], z_send.at[0], z_recv.at[0], target_device),
        remote(wout, readout_weights.at[core], z_send.at[1], z_recv.at[1], target_device),
    ]
    own_copies = [
        pltpu.make_async_copy(win, weights.at[core], z_local.at[0]),
        pltpu.make_async_copy(wout, readout_weights.at[core], z_local.at[1]),
    ]

    @pl.when(hop != 0)
    def _():
        for one in z_copies:
            one.start()

    @pl.when(hop == 0)
    def _():
        for one in own_copies:
            one.start()

    def in_copy(kind, source, slot, device):
        return remote(source, arrived.at[kind, :, slot], in_send.at[kind, slot], in_recv.at[kind, slot], device)

    def send_inputs(i, carry):
        index, device = peer(i)
        for kind in range(2):
            remote(
                patches.at[shard(index, kind)], arrived.at[kind, :, me], in_send.at[kind, index], in_recv.at[kind, me], device
            ).start()
        return carry

    lax.fori_loop(1, 16, send_inputs, 0)
    for kind in range(2):
        arrived[kind, :, me] = patches[shard(me, kind)]

    wide[...] = jnp.zeros(wide.shape, BF)
    recur = []
    for t in range(4):
        rows[t] = states[:, 128 * t : 128 * t + 128]
    for p in range(2):
        before = jnp.concatenate([rows[t, pl.ds(p, 16, stride=2), :] for t in range(4)], axis=1).astype(BF)
        recur.append(jnp.dot(before, wrec[...], preferred_element_type=F32) + bias[...])

    @pl.when(hop != 0)
    def _():
        for one in z_copies:
            one.wait()

    @pl.when(hop == 0)
    def _():
        for one in own_copies:
            one.wait()

    d2d_copies = [
        remote(weights.at[core], weights.at[core], d2d_send.at[0], d2d_recv.at[0], other_core),
        remote(readout_weights.at[core], readout_weights.at[core], d2d_send.at[1], d2d_recv.at[1], other_core),
    ]
    for one in d2d_copies:
        one.start()
    for one in d2d_copies:
        one.wait()

    for kind in range(2):
        tails = []
        for y in range(9):
            block = weights[kind, y]
            wide[10 * kind + y, 0:72, 0:512] = block
            wide[10 * kind + y, 64:128, 512:1024] = block[0:64]
            tails.append(block[64:72].astype(F32))
        tails.append(jnp.zeros((56, 512), F32))
        wide[10 * kind + 9, :, 512:1024] = jnp.concatenate(tails, axis=0).astype(BF)

    def wait_inputs(i, carry):
        index, device = peer(i)
        for kind in range(2):
            remote(
                patches.at[0], arrived.at[kind, :, index], in_send.at[kind, index], in_recv.at[kind, index], device
            ).wait()
        return carry

    lax.fori_loop(1, 16, wait_inputs, 0)
    left_side = jnp.concatenate([arrived[kind, y].reshape(256, 128) for kind in range(2) for y in range(10)], axis=1)
    for n in range(4):
        right_side = wide[:, :, 256 * n : 256 * n + 256].reshape(2560, 256)
        part = jnp.dot(left_side, right_side, preferred_element_type=F32)
        partial[:, :, 256 * n : 256 * n + 256] = part.astype(BF).reshape(16, 16, 256)

    def send_drives(i, carry):
        index, device = peer(i)
        remote(partial.at[index], partials.at[me], drive_send.at[index], drive_recv.at[me], device).start()
        return carry

    lax.fori_loop(1, 16, send_drives, 0)
    partials[me] = partial[me]

    def wait_drives(i, carry):
        index, device = peer(i)
        remote(partial.at[index], partials.at[index], drive_send.at[index], drive_recv.at[index], device).wait()
        return carry

    lax.fori_loop(1, 16, wait_drives, 0)
    drive = partials[0].astype(F32)
    for index in range(1, 16):
        drive = drive + partials[index].astype(F32)
    for p in range(2):
        state = jnp.tanh(drive[:, 512 * p : 512 * p + 512] + recur[p])
        for t in range(4):
            rows[t, pl.ds(p, 16, stride=2), :] = state[:, 128 * t : 128 * t + 128]
        mine[p] = state.astype(BF)
    for t in range(4):
        fresh[:, 128 * t : 128 * t + 128] = rows[t]

    def send_readin(i, carry):
        index, device = peer(i)
        remote(mine, readin.at[:, me], readin_send.at[index], readin_recv.at[me], device).start()
        return carry

    lax.fori_loop(1, 16, send_readin, 0)
    readin[:, me] = mine[...]

    def wait_readin(i, carry):
        index, device = peer(i)
        remote(mine, readin.at[:, index], readin_send.at[index], readin_recv.at[index], device).wait()
        return carry

    lax.fori_loop(1, 16, wait_readin, 0)
    half = lane_index(256) < 64
    for kind in range(2):
        out = [
            jnp.dot(readin[p].reshape(256, 512), readout_weights[kind], preferred_element_type=F32) for p in range(2)
        ]
        for pair in range(2):
            even, odd = (value[:, 128 * pair : 128 * pair + 128] for value in out)
            first = jnp.where(half, even, pltpu.roll(odd, 64, 1))
            second = jnp.where(half, pltpu.roll(even, 64, 1), odd)
            pieces[:, kind, 2 * pair] = first.astype(BF).reshape(16, 16, 128)
            pieces[:, kind, 2 * pair + 1] = second.astype(BF).reshape(16, 16, 128)

    def send_out(i, carry):
        index, device = peer(i)
        for kind in range(2):
            remote(
                pieces.at[index, kind], returned.at[shard(me, kind)], out_send.at[kind, index], out_recv.at[kind, me], device
            ).start()
        return carry

    lax.fori_loop(1, 16, send_out, 0)
    for kind in range(2):
        returned[shard(me, kind)] = pieces[me, kind]

    def wait_out(i, carry):
        index, device = peer(i)
        for kind in range(2):
            remote(
                pieces.at[index, kind], returned.at[shard(index, kind)], out_send.at[kind, index], out_recv.at[kind, index], device
            ).wait()
        return carry

    lax.fori_loop(1, 16, wait_out, 0)
    for ch in range(2):

        def place(k, carry):
            for y in range(4):
                tile = returned[16 * ch + k, y].astype(F32)
                placed[ch, pl.ds(4 * k + y, 16, stride=64), :] = tile
            return carry

        lax.fori_loop(0, 16, place, 0)
        for a in range(4):
            for j in range(4):
                at = (slice(64 * a, 64 * a + 64), slice(128 * j, 128 * j + 128))
                base = 64 * (4 * a + j)
                prediction[(ch, *at)] = gain[ch] * model[(ch, *at)] + placed[ch, base : base + 64, :]


def reservoir(patches, model, win, wout, wrec, bias, states, gain):
    vmem = pl.BlockSpec(memory_space=pltpu.VMEM)
    hbm = pl.BlockSpec(memory_space=pl.ANY)
    dma = pltpu.SemaphoreType.DMA
    return pl.pallas_call(
        reservoir_kernel,
        name="reservoir",
        out_shape=(
            jax.ShapeDtypeStruct((2, 256, 512), F32),
            jax.ShapeDtypeStruct((32, 512), F32),
        ),
        in_specs=[vmem, vmem, hbm, hbm, vmem, vmem, vmem, vmem],
        out_specs=(vmem, vmem),
        scratch_shapes=[
            pltpu.VMEM((4, 32, 128), F32),
            pltpu.VMEM((2, 9, 72, 512), BF),
            pltpu.VMEM((20, 128, 1024), BF),
            pltpu.VMEM((2, 512, 256), BF),
            pltpu.VMEM((2, 10, 16, 16, 128), BF),
            pltpu.VMEM((16, 16, 1024), BF),
            pltpu.VMEM((16, 16, 1024), BF),
            pltpu.VMEM((2, 16, 512), BF),
            pltpu.VMEM((2, 16, 16, 512), BF),
            pltpu.VMEM((16, 2, 4, 16, 128), BF),
            pltpu.VMEM((32, 4, 16, 128), BF),
            pltpu.VMEM((2, 1024, 128), F32),
            dma((2,)), dma((2,)), dma((2,)),
            dma((2,)), dma((2,)),
            dma((2, 16)), dma((2, 16)),
            dma((16,)), dma((16,)),
            dma((16,)), dma((16,)),
            dma((2, 16)), dma((2, 16)),
        ],
        compiler_params=pltpu.CompilerParams(collective_id=1, has_side_effects=True, vmem_limit_bytes=48 << 20),
    )(patches, model, win, wout, wrec, bias, states, gain)


def local(field, states, input_weight, recurrent_weight, bias, output_weight, model_gain):
    patches, model = forecast(field)
    gain = jnp.concatenate([model_gain, model_gain], axis=2)
    prediction, fresh = reservoir(
        patches, model, input_weight.reshape(9, PATCH, NODES), output_weight, recurrent_weight,
        bias.reshape(1, NODES), states.reshape(32, NODES), gain,
    )
    return prediction, fresh.reshape(4, 8, NODES)


def solution(mesh):
    placed = (
        P(None, "row", "col"),
        P("row", "col", None),
        P("col", None),
        P(),
        P(),
        P(None, "col"),
        P(),
    )
    return jax.shard_map(
        local, mesh=mesh, in_specs=placed, out_specs=(P(None, "row", "col"), P("row", "col", None)), check_vma=False
    )
```

time: 254 us -> 104 us (0.41)
  Pallas kernels: 0 us -> 95.5 us
  waiting for transfers between devices: 87.4 us -> 0 us
  blocking collectives: 47.8 us -> 0 us
  starting transfers between devices: 39.9 us -> 0 us
  local copies, waits for them, and re-layouts: 40 us -> 6.61 us
  between operations: 14.4 us -> 0.7 us
  other arithmetic: 14.7 us -> 1.05 us
  matrix products: 8.39 us -> 0 us
    pallas_call x0 -> x2, Pallas kernels: none -> 95.5 us  [the longest x1 67.6 us: reservoir(): pl.pallas_call(reservoir_kernel, name='reservoir', out_shape=(jax.ShapeDt...]
    all_to_all x1 -> x0, blocking collectives: 47.8 us -> none  [local(): lax.all_to_all(inputs, 'col', split_axis=1, concat_axis=0, tiled=True)]
    all_to_all x1 -> x0, waiting for transfers between devices: 45.7 us -> none  [sum_at_owner(): lax.all_to_all(parts, axis, split_axis=0, concat_axis=0, tiled=True)]
    ppermute x20 -> x0, waiting for transfers between devices: 41 us -> none  [the longest x8 31 us: extended(): lax.ppermute(last, axis, up)]
    ppermute x20 -> x0, starting transfers between devices: 34.9 us -> none  [the longest x8 18.5 us: extended(): lax.ppermute(leading, axis, [(b, a) for a, b in up])]
    another operation x33 -> x0, local copies, waits for them, and re-layouts: 26.7 us -> none  [local(): inputs = jnp.stack(pieces).reshape(count, -1).astype(jnp.bfloat16)]
    dot_general x3 -> x0, matrix products: 8.39 us -> none  [the longest x1 5.9 us: local(): jnp.dot(readin, lax.all_gather(output_weight, 'col', axis=1, tiled=True),...]
    sub x8 -> x0, other arithmetic: 7.27 us -> none  [the longest x4 6.1 us: shrunk_tendency(): padded[:, :-2, 1:-1] + padded[:, 2:, 1:-1] + padded[:, 1:-1, :-2]]
  transfers between devices with their start and end apart: 22 -> 0, of which waited for: 9 -> 0; matrix products, arithmetic and copies ran while one was open for 19% -> 0% of each run, Pallas kernels for 0% -> 0%
where the time goes in v1:
time: 104 us
  Pallas kernels  95.5 us (92%)
  local copies, waits for them, and re-layouts  6.61 us (6%)
  other arithmetic  1.05 us (1%)
    pallas_call x1, Pallas kernels, reservoir(): pl.pallas_call(reservoir_kernel, name='reservoir', out_shape=(jax.ShapeDt...  67.6 us
    pallas_call x1, Pallas kernels, forecast(): pl.pallas_call(forecast_kernel, name='forecast', out_shape=(jax.ShapeDtyp...  27.9 us
    unnamed x16, local copies, waits for them, and re-layouts  6.61 us

profile of v1, /device:TPU:1, one launch (start us, length us, event | category | flops | bytes accessed | tf_op | source)
XLA Modules:
  0.0 103.9 jit_solution(2747507141091946731)
XLA Ops:
  0.6 0.0 copy-start.3
  0.6 0.0 copy-start.2
  0.7 1.0 %pad_maximum_fusion.gain = f32[2,64,128]{2,1,0:T(8,128)S(1)} fusion(f32[2,64,64]{2,1,0:T(8,128)} %param.13), kind=kLoop, calls=%fused_computation | loop fusion | flops 16384 | bytes 98304 | tf_op jit(solution)/shard_map/concatenate | solution.py:476
  1.7 27.9 %forecast.1 = (bf16[32,10,16,128]{3,2,1,0:T(8,128)(2,1)}, f32[2,256,512]{2,1,0:T(8,128)}) custom-call(f32[2,256,512]{2,1,0:T(8,128)} %field.1), custom_call_target="tpu_custom_call" | custom-call | tf_op jit(solution)/shard_map/forecast/pallas_call | solution.py:187
  29.6 0.0 copy-done.3
  29.6 0.0 copy-done.2
  29.6 0.0 copy-start
  29.7 1.3 %copy-done = bf16[32,10,16,128]{3,2,1,0:T(8,128)(2,1)S(1)} copy-done((bf16[32,10,16,128]{3,2,1,0:T(8,128)(2,1)S(1)}, bf16[32,10,16,128]{3,2,1,0:T(8,128)(2,1)}, u32[]{:S(2)}) %copy-start) | copy-done | bytes 1310744
  31.0 0.0 copy-start.1
  31.0 1.2 %copy-done.1 = f32[2,256,512]{2,1,0:T(8,128)S(1)} copy-done((f32[2,256,512]{2,1,0:T(8,128)S(1)}, f32[2,256,512]{2,1,0:T(8,128)}, u32[]{:S(2)}) %copy-start.1) | copy-done | bytes 1048600
  32.2 0.0 copy-start.4
  32.2 0.9 copy-done.4
  33.1 0.0 copy-start.5
  33.1 0.8 copy-done.5
  34.0 0.0 copy-start.6
  34.0 0.7 copy-done.6
  34.7 67.6 %reservoir.1 = (f32[2,256,512]{2,1,0:T(8,128)S(1)}, f32[32,512]{1,0:T(8,128)S(1)}) custom-call(bf16[32,10,16,128]{3,2,1,0:T(8,128)(2,1)S(1)} %copy-done, f32[2,256,512]{2,1,0:T(8,128)S(1)} %copy-done.1, bf16[9,72,512]{2,1,0:T(8,128)(2,1)S(1)} %bitcast.4, bf16[512,256]{1,0:T(8,128)(2,1)S(1)} %copy-done.4, bf16[512,512]{1,0:T(8,128)(2,1)S(1)} %copy-done.3, ...), custom_call_target="tpu_custom_call" | custom-call | tf_op jit(solution)/shard_map/reservoir/pallas_call | solution.py:441
  102.3 1.0 copy.11
  103.3 0.6 copy.12
Async XLA Ops:
  0.6 29.0 %copy-start.3 = (bf16[512,512]{1,0:T(8,128)(2,1)S(1)}, bf16[512,512]{1,0:T(8,128)(2,1)}, u32[]{:S(2)}) copy-start(bf16[512,512]{1,0:T(8,128)(2,1)} %wrec.1) | copy-start | bytes 1572868
  0.6 29.0 %copy-start.2 = (bf16[648,512]{1,0:T(8,128)(2,1)S(1)}, bf16[648,512]{1,0:T(8,128)(2,1)}, u32[]{:S(2)}) copy-start(bf16[648,512]{1,0:T(8,128)(2,1)} %param.9) | copy-start | bytes 1990660
  29.6 1.3 %copy-start = (bf16[32,10,16,128]{3,2,1,0:T(8,128)(2,1)S(1)}, bf16[32,10,16,128]{3,2,1,0:T(8,128)(2,1)}, u32[]{:S(2)}) copy-start(bf16[32,10,16,128]{3,2,1,0:T(8,128)(2,1)} %get-tuple-element.6.patches) | copy-start | bytes 3932164
  31.0 1.2 %copy-start.1 = (f32[2,256,512]{2,1,0:T(8,128)S(1)}, f32[2,256,512]{2,1,0:T(8,128)}, u32[]{:S(2)}) copy-start(f32[2,256,512]{2,1,0:T(8,128)} %get-tuple-element.7.model) | copy-start | bytes 3145732
  32.2 0.9 copy-start.4
  33.1 0.8 copy-start.5
  34.0 0.7 copy-start.6
